TPU v7x, 32 devices: a whole 2x2x4 slice. The times are simulated.
32 devices in a mesh: expert: 4 (over z), tensor: 8 (over y, x, core).
Axes of the slice: x: 2, y: 2, z: 4, core: 2. Of those that a mesh axis runs over, the one named last changes fastest.
Arguments:
- stashed: bfloat16 [384, 4096], P('expert', 'tensor'), may hold values from -6 to 6
- expert_ids: int32 [384, 2], P('expert'), may hold values from 0 to 3, all different within a row; in each aligned block of 96 rows (0 to 95, 96 to 191, ...) at most 64 rows name the same one
- combine_weight: float32 [384, 2], P('expert'), may hold values from 0.2 to 1
- w_gate: bfloat16 [4, 7168, 4096], P('expert', 'tensor'), may hold values from -0.09375 to 0.09375
- w_up: bfloat16 [4, 7168, 4096], P('expert', 'tensor'), may hold values from -0.09375 to 0.09375
- w_down: bfloat16 [4, 7168, 4096], P('expert', 'tensor'), may hold values from -0.09375 to 0.09375
Outputs:
- mixed_out: bfloat16 [384, 4096], P('expert', 'tensor')
Inputs may be any that keep to these rules, and one draw needn't show every extreme that they name: `expert_ids`: each row names two different experts. Among the 96 rows of one group (aligned blocks) no expert is named more than 64 times, and in some group some expert is named exactly 64 times.
All inputs are finite; a program needn't handle non-finite values.
Results may differ from a plain program's by a relative error of at most 0.0049.
Values may be sent and summed in bfloat16 or wider, within the bound.
A program may use at most 64 MiB of HBM per device.

v0:
```python
import jax
import jax.numpy as jnp
from jax import lax
from jax.sharding import PartitionSpec as P


def slot_targets(expert_ids, experts, capacity):
    flat_ids = expert_ids.reshape(-1)
    one_hot = (flat_ids[:, None] == jnp.arange(experts, dtype=jnp.int32)[None, :]).astype(jnp.int32)
    before = jnp.cumsum(one_hot, axis=0) - one_hot
    slot_index = jnp.sum(before * one_hot, axis=1)
    return (flat_ids * capacity + slot_index).reshape(expert_ids.shape)


def contract_last(left, right):
    return lax.dot_general(
        left, right, (((1,), (1,)), ((), ())), preferred_element_type=jnp.float32
    )


def shards(stashed, expert_ids, combine_weight, w_gate, w_up, w_down):
    tok_count = stashed.shape[0]
    feat_width = stashed.shape[1]
    experts = lax.axis_size("expert")
    capacity = min(tok_count, 8 * tok_count // (3 * experts))
    targets = slot_targets(expert_ids, experts, capacity)
    columns = jnp.arange(experts * capacity, dtype=jnp.int32)
    pair_match = (targets[:, :, None] == columns[None, None, :]).astype(jnp.float32)
    selector = jnp.sum(pair_match, axis=1).T.astype(jnp.bfloat16)
    mixing = jnp.sum(pair_match * combine_weight[:, :, None], axis=1)
    gate_w = w_gate[0]
    up_w = w_up[0]
    down_w = w_down[0]
    gathered = lax.all_gather(stashed, "tensor", axis=1, tiled=True)
    outgoing = jnp.dot(selector, gathered, preferred_element_type=jnp.float32).astype(jnp.bfloat16)
    outgoing = outgoing.reshape(experts, capacity, gathered.shape[1])
    received = lax.all_to_all(outgoing, "expert", split_axis=0, concat_axis=0, tiled=True)
    sources, item_count, full_width = received.shape
    rows_in = received.reshape(sources * item_count, full_width)
    gate_acts = contract_last(rows_in, gate_w)
    up_acts = contract_last(rows_in, up_w)
    hidden = (jax.nn.silu(gate_acts) * up_acts).astype(jnp.bfloat16)
    result = jnp.dot(hidden, down_w, preferred_element_type=jnp.float32)
    partial_value = result.reshape(sources, item_count, result.shape[1])
    partial_value = partial_value.reshape(-1, partial_value.shape[2])
    own_share = lax.psum_scatter(partial_value, "tensor", scatter_dimension=1, tiled=True)
    returned_rows = lax.all_to_all(
        own_share.reshape(experts, capacity, feat_width),
        "expert",
        split_axis=0,
        concat_axis=0,
        tiled=True,
    )
    combined = jnp.dot(
        mixing,
        returned_rows.reshape(experts * capacity, feat_width),
        precision=lax.Precision.HIGHEST,
        preferred_element_type=jnp.float32,
    )
    return combined.astype(jnp.bfloat16)


def solution(mesh):
    return jax.shard_map(
        shards,
        mesh=mesh,
        in_specs=(
            P("expert", "tensor"),
            P("expert", None),
            P("expert", None),
            P("expert", "tensor", None),
            P("expert", "tensor", None),
            P("expert", "tensor", None),
        ),
        out_specs=P("expert", "tensor"),
        check_vma=False,
    )
```

profile of v0, /device:TPU:0, one launch (start us, length us, event | category | flops | bytes accessed | tf_op | source)
XLA Modules:
  0.0 167.9 jit_solution(18047453095320567481)
XLA Ops:
  6.5 0.0 reduce-scatter.2.cloned.1.call-start
  6.5 0.8 copy.23
  7.3 0.1 eq.35
  7.5 1.2 reduce-window.6
  8.7 0.1 slice.12
  8.8 0.1 copy.24
  8.9 0.1 copy.25
  9.0 0.1 add_bitcast_fusion
  9.1 0.1 reduce_sum.30
  9.3 0.1 copy.26
  9.3 0.0 copy-start
  9.3 0.9 multiply_add_fusion
  10.2 12.5 %all_gather.3 = bf16[96,4096]{1,0:T(8,128)(2,1)S(1)} all-gather(bf16[96,512]{1,0:T(8,128)(2,1)} %param.6), channel_id=1, replica_groups=mesh['expert'=4,'tensor'=8] {'tensor'}, dimensions={1}, use_global_device_ids=true | all-gather | bytes 884736 | tf_op jit(solution)/shard_map/all_gather | solution.py:34
  22.7 0.8 convert_reduce_fusion
  23.5 0.7 convolution_convert_fusion
  24.2 53.4 %all_to_all.10 = bf16[4,64,4096]{2,1,0:T(8,128)(2,1)S(1)} all-to-all(bf16[4,64,4096]{2,1,0:T(8,128)(2,1)S(1)} %bitcast.34), channel_id=1, replica_groups=mesh['expert'=4,'tensor'=8] {'expert'}, dimensions={0} | all-to-all | bytes 4194304 | tf_op jit(solution)/shard_map/all_to_all | solution.py:37
  77.6 0.0 copy-done
  77.6 2.4 %fusion.4 = f32[256,896]{1,0:T(8,128)S(1)} fusion(bf16[256,4096]{1,0:T(8,128)(2,1)S(1)} %bitcast.35, bf16[1,896,4096]{2,1,0:T(8,128)(2,1)S(1)} %copy-done), kind=kOutput, calls=%fused_computation.4 | convolution fusion | flops 1879048192 | bytes 10354688 | tf_op jit(solution)/shard_map/dot_general | solution.py:16
  80.0 11.7 %fusion = f32[256,4096]{1,0:T(8,128)} fusion(bf16[1,896,4096]{2,1,0:T(8,128)(2,1)} %param.11, bf16[256,4096]{1,0:T(8,128)(2,1)S(1)} %bitcast.36, bf16[1,896,4096]{2,1,0:T(8,128)(2,1)} %param.10, f32[256,896]{1,0:T(8,128)S(1)} %fusion.4), kind=kOutput, calls=%fused_computation | convolution fusion | flops 3759472640 | bytes 21889024 | tf_op jit(solution)/shard_map/dot_general | solution.py:43
  91.7 0.0 reduce-scatter.2.cloned.1.call-update
  91.7 49.4 %reduce-scatter.2.cloned.1.call-done = f32[256,512]{1,0:T(8,128)} async-done(((f32[256,4096]{1,0:T(8,128)}), f32[256,512]{1,0:T(8,128)}) %reduce-scatter.2.cloned.1.call-update) | async-done | bytes 524304 | tf_op jit(solution)/shard_map/reduce_scatter | solution.py:46
  141.1 18.9 %all_to_all.11 = f32[4,64,512]{2,1,0:T(8,128)S(1)} all-to-all(f32[4,64,512]{2,1,0:T(8,128)} %bitcast.38), channel_id=1, replica_groups=mesh['expert'=4,'tensor'=8] {'expert'}, dimensions={0} | all-to-all | bytes 1048576 | tf_op jit(solution)/shard_map/all_to_all | solution.py:47
  160.0 1.1 convolution_convert_fusion.1
  (7 shorter events, 0.1 us)
Async XLA Ops:
  6.5 134.6 %reduce-scatter.2.cloned.1.call-start = ((), (), s32[]{:S(2)}) async-start(), calls=%async_computation.3 | async-start | bytes 4718592 | tf_op jit(solution)/shard_map/reduce_scatter | solution.py:46
  9.3 68.3 %copy-start = (bf16[1,896,4096]{2,1,0:T(8,128)(2,1)S(1)}, bf16[1,896,4096]{2,1,0:T(8,128)(2,1)}, u32[]{:S(2)}) copy-start(bf16[1,896,4096]{2,1,0:T(8,128)(2,1)} %param.9) | copy-start | bytes 22020100
Sparse Core Ops, SparseCore 0:
  91.8 49.2 reduce-scatter.1
where the time goes:
time: 168 us
  blocking collectives  84.8 us (50%)
  waiting for transfers between devices  49.4 us (29%)
  matrix products  15.9 us (9%)
  between operations  13.4 us (8%)
  other arithmetic  3.03 us (2%)
    all_to_all x1, blocking collectives, shards(): lax.all_to_all(outgoing, 'expert', split_axis=0, concat_axis=0, tiled=True)  53.4 us
    reduce_scatter x1, waiting for transfers between devices, shards(): lax.psum_scatter(partial_value, 'tensor', scatter_dimension=1, tiled=True)  49.4 us
    all_to_all x1, blocking collectives, shards(): lax.all_to_all(own_share.reshape(experts, capacity, feat_width), 'expert'...  18.9 us
    all_gather x1, blocking collectives, shards(): gathered = lax.all_gather(stashed, 'tensor', axis=1, tiled=True)  12.5 us
    dot_general x1, matrix products, shards(): result = jnp.dot(hidden, down_w, preferred_element_type=jnp.float32)  11.7 us
  transfers between devices with their start and end apart: 1, of which 1 were waited for; matrix products, arithmetic and copies ran while one was open for 0% of the time, Pallas kernels for 0%

commit v1 on v0

--- a/solution.py
+++ b/solution.py
@@ -34,7 +34,15 @@
     gathered = lax.all_gather(stashed, "tensor", axis=1, tiled=True)
     outgoing = jnp.dot(selector, gathered, preferred_element_type=jnp.float32).astype(jnp.bfloat16)
     outgoing = outgoing.reshape(experts, capacity, gathered.shape[1])
-    received = lax.all_to_all(outgoing, "expert", split_axis=0, concat_axis=0, tiled=True)
+    ways, here = (lax.axis_size("expert"), lax.axis_index("expert"))
+    width = outgoing.shape[0] // ways
+    turned = jnp.roll(outgoing, -here * width, axis=0)
+    got = [lax.slice_in_dim(turned, 0, width, axis=0)]
+    for far in range(1, ways):
+        sent = lax.slice_in_dim(turned, far * width, (far + 1) * width, axis=0)
+        got.append(lax.ppermute(sent, "expert", [(d, (d + far) % ways) for d in range(ways)]))
+    line = jnp.concatenate(got[::-1], axis=0)
+    received = jnp.roll(line, (here + 1) * got[0].shape[0], axis=0)
     sources, item_count, full_width = received.shape
     rows_in = received.reshape(sources * item_count, full_width)
     gate_acts = contract_last(rows_in, gate_w)

time: 168 us -> 175 us (1.042)
  blocking collectives: 84.8 us -> 31.1 us
  waiting for transfers between devices: 49.4 us -> 94 us
  starting transfers between devices: 0.01 us -> 5.52 us
  other arithmetic: 3.03 us -> 7.21 us
  matrix products: 15.9 us -> 18.9 us
  local copies, waits for them, and re-layouts: 1.42 us -> 4 us
    all_to_all x1 -> x0, blocking collectives: 53.4 us -> none  [shards(): lax.all_to_all(outgoing, 'expert', split_axis=0, concat_axis=0, tiled=True)]
    ppermute x0 -> x3, waiting for transfers between devices: none -> 33.3 us  [shards(): lax.ppermute(sent, 'expert', [(d, (d + far) % ways) for d in range(ways)])]
    reduce_scatter x1, waiting for transfers between devices: 49.4 us -> 60.7 us  [shards(): lax.psum_scatter(partial_value, 'tensor', scatter_dimension=1, tiled=True)]
    ppermute x0 -> x3, starting transfers between devices: none -> 5.52 us  [shards(): lax.ppermute(sent, 'expert', [(d, (d + far) % ways) for d in range(ways)])]
    concatenate x0 -> x2, other arithmetic: none -> 4.32 us  [the longest x1 3.56 us: shards(): received = jnp.roll(line, (here + 1) * got[0].shape[0], axis=0)]
    dot_general x1, matrix products: 2.36 us -> 5.44 us  [contract_last(): lax.dot_general(left, right, (((1,), (1,)), ((), ())), preferred_element_...]
  transfers between devices with their start and end apart: 1 -> 4, of which waited for: 1 -> 3; matrix products, arithmetic and copies ran while one was open for 0% -> 0% of each run, Pallas kernels for 0% -> 0%
where the time goes in v1:
time: 175 us; the launch traced here: 174 us
  waiting for transfers between devices  94 us (54%)
  blocking collectives  31.1 us (18%)
  matrix products  18.9 us (11%)
  between operations  13.5 us (8%)
  other arithmetic  7.21 us (4%)
  starting transfers between devices  5.52 us (3%)
  local copies, waits for them, and re-layouts  4 us (2%)
    reduce_scatter x1, waiting for transfers between devices, shards(): lax.psum_scatter(partial_value, 'tensor', scatter_dimension=1, tiled=True)  60.7 us
    ppermute x3, waiting for transfers between devices, shards(): lax.ppermute(sent, 'expert', [(d, (d + far) % ways) for d in range(ways)])  33.3 us
    all_to_all x1, blocking collectives, shards(): lax.all_to_all(own_share.reshape(experts, capacity, feat_width), 'expert'...  18.9 us
    all_gather x1, blocking collectives, shards(): gathered = lax.all_gather(stashed, 'tensor', axis=1, tiled=True)  12.2 us
    dot_general x1, matrix products, shards(): result = jnp.dot(hidden, down_w, preferred_element_type=jnp.float32)  11.7 us
    ppermute x3, starting transfers between devices, shards(): lax.ppermute(sent, 'expert', [(d, (d + far) % ways) for d in range(ways)])  5.52 us
    dot_general x1, matrix products, contract_last(): lax.dot_general(left, right, (((1,), (1,)), ((), ())), preferred_element_...  5.44 us
    concatenate x1, other arithmetic, shards(): received = jnp.roll(line, (here + 1) * got[0].shape[0], axis=0)  3.56 us
  transfers between devices with their start and end apart: 4, of which 3 were waited for; matrix products, arithmetic and copies ran while one was open for 0% of the time, Pallas kernels for 0%

profile of v1, /device:TPU:0, one launch (start us, length us, event | category | flops | bytes accessed | tf_op | source)
XLA Modules:
  0.0 174.2 jit_solution(1134631223924943389)
XLA Ops:
  6.5 0.0 reduce-scatter.2.cloned.1.call-start
  6.5 0.8 copy.23
  7.3 0.1 eq.37
  7.5 1.2 reduce-window.6
  8.7 0.1 slice.28
  8.8 0.1 copy.24
  8.9 0.1 copy.25
  9.0 0.1 add_bitcast_fusion
  9.1 0.1 reduce_sum.30
  9.3 0.1 copy.26
  9.3 0.7 multiply_add_fusion
  10.1 12.2 %all_gather.3 = bf16[96,4096]{1,0:T(8,128)(2,1)S(1)} all-gather(bf16[96,512]{1,0:T(8,128)(2,1)} %param.8), channel_id=1, replica_groups=mesh['expert'=4,'tensor'=8] {'tensor'}, dimensions={1}, use_global_device_ids=true | all-gather | bytes 884736 | tf_op jit(solution)/shard_map/all_gather | solution.py:34
  22.3 0.8 convert_reduce_fusion
  23.1 0.7 convolution_convert_fusion
  23.8 0.8 fusion.13
  24.6 1.0 fusion.23
  25.6 1.6 collective-permute-start.2
  27.1 2.6 %collective-permute-start.1 = (bf16[1,64,4096]{2,1,0:T(8,128)(2,1)S(1)}, bf16[1,64,4096]{2,1,0:T(8,128)(2,1)S(1)}, u32[]{:S(2)}, u32[]{:S(2)}) collective-permute-start(bf16[1,64,4096]{2,1,0:T(8,128)(2,1)S(1)} %get-tuple-element.10), channel_id=1, source_target_pairs={{0,16},{8,24},{16,0},{24,8},{1,17},{9,25},{17,1},{25,9},{2,18},{10... | collective-permute-start | bytes 1572872 | tf_op jit(solution)/shard_map/ppermute | solution.py:43
  29.7 1.3 collective-permute-start
  31.1 11.4 %collective-permute-done.2 = bf16[1,64,4096]{2,1,0:T(8,128)(2,1)S(1)} collective-permute-done((bf16[1,64,4096]{2,1,0:T(8,128)(2,1)}, bf16[1,64,4096]{2,1,0:T(8,128)(2,1)S(1)}, u32[]{:S(2)}, u32[]{:S(2)}) %collective-permute-start.2) | collective-permute-done | bytes 524320 | tf_op jit(solution)/shard_map/ppermute | solution.py:43
  42.5 21.9 %collective-permute-done.1 = bf16[1,64,4096]{2,1,0:T(8,128)(2,1)S(1)} collective-permute-done((bf16[1,64,4096]{2,1,0:T(8,128)(2,1)S(1)}, bf16[1,64,4096]{2,1,0:T(8,128)(2,1)S(1)}, u32[]{:S(2)}, u32[]{:S(2)}) %collective-permute-start.1) | collective-permute-done | bytes 524320 | tf_op jit(solution)/shard_map/ppermute | solution.py:43
  64.4 0.0 copy-start
  64.4 0.0 collective-permute-done
  64.4 0.8 copy-done
  65.2 0.0 copy-start.1
  65.2 0.8 copy-done.1
  66.0 3.6 %fusion.9 = bf16[4,64,4096]{2,1,0:T(8,128)(2,1)S(1)} fusion(s32[]{:T(128)S(6)} %select_n.15, bf16[1,64,4096]{2,1,0:T(8,128)(2,1)} %copy-done.1, bf16[1,64,4096]{2,1,0:T(8,128)(2,1)} %copy-done, bf16[1,64,4096]{2,1,0:T(8,128)(2,1)S(1)} %collective-permute-done.2, bf16[1,64,4096]{2,1,0:T(8,128)(2,1)S(1)} %get-tuple-element.8), kind=kLoop, calls=%fused_computation.20 | loop fusion | flops 7340032 | bytes 4194308 | tf_op jit(solution)/shard_map/jit(_roll_dynamic)/concatenate | solution.py:45
  69.6 5.4 %fusion.2 = f32[256,896]{1,0:T(8,128)S(1)} fusion(bf16[256,4096]{1,0:T(8,128)(2,1)S(1)} %bitcast.33, bf16[1,896,4096]{2,1,0:T(8,128)(2,1)} %param.12), kind=kOutput, calls=%fused_computation.2 | convolution fusion | flops 1879048192 | bytes 10354688 | tf_op jit(solution)/shard_map/dot_general | solution.py:16
  75.0 11.7 %fusion = f32[256,4096]{1,0:T(8,128)} fusion(bf16[1,896,4096]{2,1,0:T(8,128)(2,1)} %param.13, f32[256,896]{1,0:T(8,128)S(1)} %fusion.2, bf16[256,4096]{1,0:T(8,128)(2,1)S(1)} %bitcast.34, bf16[1,896,4096]{2,1,0:T(8,128)(2,1)} %param.11), kind=kOutput, calls=%fused_computation | convolution fusion | flops 3759472640 | bytes 21889024 | tf_op jit(solution)/shard_map/dot_general | solution.py:51
  86.7 0.0 reduce-scatter.2.cloned.1.call-update
  86.7 60.7 %reduce-scatter.2.cloned.1.call-done = f32[256,512]{1,0:T(8,128)} async-done(((f32[256,4096]{1,0:T(8,128)}), f32[256,512]{1,0:T(8,128)}) %reduce-scatter.2.cloned.1.call-update) | async-done | bytes 524304 | tf_op jit(solution)/shard_map/reduce_scatter | solution.py:54
  147.4 18.9 %all_to_all.5 = f32[4,64,512]{2,1,0:T(8,128)S(1)} all-to-all(f32[4,64,512]{2,1,0:T(8,128)} %bitcast.36), channel_id=1, replica_groups=mesh['expert'=4,'tensor'=8] {'expert'}, dimensions={0} | all-to-all | bytes 1048576 | tf_op jit(solution)/shard_map/all_to_all | solution.py:55
  166.3 1.1 convolution_convert_fusion.1
  (7 shorter events, 0.1 us)
Async XLA Ops:
  6.5 140.9 %reduce-scatter.2.cloned.1.call-start = ((), (), s32[]{:S(2)}) async-start(), calls=%async_computation.2 | async-start | bytes 4718592 | tf_op jit(solution)/shard_map/reduce_scatter | solution.py:54
  25.6 16.9 %collective-permute-start.2 = (bf16[1,64,4096]{2,1,0:T(8,128)(2,1)}, bf16[1,64,4096]{2,1,0:T(8,128)(2,1)S(1)}, u32[]{:S(2)}, u32[]{:S(2)}) collective-permute-start(bf16[1,64,4096]{2,1,0:T(8,128)(2,1)} %get-tuple-element.9), channel_id=1, source_target_pairs={{0,8},{8,16},{16,24},{24,0},{1,9},{9,17},{17,25},{25,1},{2,10},{10... | collective-permute-start | bytes 1572872 | tf_op jit(solution)/shard_map/ppermute | solution.py:43
  27.1 37.3 %collective-permute-start.1 = (bf16[1,64,4096]{2,1,0:T(8,128)(2,1)S(1)}, bf16[1,64,4096]{2,1,0:T(8,128)(2,1)S(1)}, u32[]{:S(2)}, u32[]{:S(2)}) collective-permute-start(bf16[1,64,4096]{2,1,0:T(8,128)(2,1)S(1)} %get-tuple-element.10), channel_id=1, source_target_pairs={{0,16},{8,24},{16,0},{24,8},{1,17},{9,25},{17,1},{25,9},{2,18},{10... | collective-permute-start | bytes 1572872 | tf_op jit(solution)/shard_map/ppermute | solution.py:43
  29.7 34.7 %collective-permute-start = (bf16[1,64,4096]{2,1,0:T(8,128)(2,1)S(1)}, bf16[1,64,4096]{2,1,0:T(8,128)(2,1)S(1)}, u32[]{:S(2)}, u32[]{:S(2)}) collective-permute-start(bf16[1,64,4096]{2,1,0:T(8,128)(2,1)S(1)} %get-tuple-element.11), channel_id=1, source_target_pairs={{0,24},{8,0},{16,8},{24,16},{1,25},{9,1},{17,9},{25,17},{2,26},{10... | collective-permute-start | bytes 1572872 | tf_op jit(solution)/shard_map/ppermute | solution.py:43
  64.4 0.8 copy-start
  65.2 0.8 copy-start.1
Sparse Core Ops, SparseCore 0:
  86.8 60.5 reduce-scatter.1
